TPU v7x, 32 devices: a whole 2x2x4 slice. The times are simulated.
32 devices in a mesh: runs: 2 (over y), gx: 4 (over z), gy: 2 (over x), gz: 2 (over core).
Axes of the slice: x: 2, y: 2, z: 4, core: 2. Of those that a mesh axis runs over, the one named last changes fastest.
Arguments:
- positions: float32 [3, 8, 4096], P(None, None, ('runs', 'gx', 'gy', 'gz')), parts along dimension 2, as said below
- velocities: float32 [3, 8, 4096], P(None, None, ('runs', 'gx', 'gy', 'gz')), parts along dimension 2, may hold values from -5 to 5
- send_list: int32 [5696], P(('runs', 'gx', 'gy', 'gz')), parts along dimension 0, may hold values from 0 to 127
- pair_list: int32 [2, 57344], P(None, ('runs', 'gx', 'gy', 'gz')), parts along dimension 1, may hold values from 0 to 306, as said below
- constraint_flags: int32 [7, 4096], P(None, ('runs', 'gx', 'gy', 'gz')), parts along dimension 1, may hold values 0 or 1
Outputs:
- final_positions: float32 [3, 8, 4096], P(None, None, ('runs', 'gx', 'gy', 'gz')), parts along dimension 2
- final_velocities: float32 [3, 8, 4096], P(None, None, ('runs', 'gx', 'gy', 'gz')), parts along dimension 2
- energies: float32 [6, 2], P('runs'), parts along dimension 0
There are 2 independent parts, one for each index of `runs`. A program takes and returns all parts, laid end to end along the dimension named above; each array names one. Nothing has to cross between parts.
Inputs may be any that keep to these rules, and one draw needn't show every extreme that they name: `pair_list`: each domain's 1792 slots name clusters of its extended set: 0 to 127 its own, then its received zone blocks in order; padding slots hold 306 in both rows; every cluster appears in a slot with itself; no unordered pair appears twice. `positions`: eight beads of a cluster lie in its cell of side 1, the cells of a domain filling a box of 1 by 8 by 16; neighbouring beads of a cluster are between 0.25 and 0.6 apart.
All inputs are finite; a program needn't handle non-finite values. No bound on the sum of `constraint_flags` on one device may be relied on, other than what follows from the above.
Results may differ from a plain program's by a relative error of at most 0.0003.
Values sent between devices are 32-bit elements; how exact they have to be, the bound alone decides.
A program may use at most 64 MiB of HBM per device.

v0:
```python
import jax
import jax.numpy as jnp
import numpy as np
from jax import lax
from jax.sharding import PartitionSpec as P

CX = 1
CY = 8
CZ = 16
ITERS = 3
NORDER = 4
time_step = 0.02
strength = 2.0
root_half = 0.7071067811865476
zone_list = ((1, 0, 0), (0, 1, 0), (0, 0, 1), (1, 1, 0), (1, 0, 1), (0, 1, 1), (1, 1, 1))


def from_behind(value, axis, by):
    count = lax.axis_size(axis)
    return lax.ppermute(value, axis, [(i, (i + by) % count) for i in range(count)])


def zone_sizes():
    return tuple(
        (
            (CX if direction[0] == 0 else 1)
            * (CY if direction[1] == 0 else 1)
            * (CZ if direction[2] == 0 else 1)
            for direction in zone_list
        )
    )


def split_blocks(packed, block_sizes):
    pieces = []
    position = 0
    for length in block_sizes:
        pieces.append(packed[:, :, position : position + length])
        position += length
    return pieces


def shell_offsets():
    block_sizes = zone_sizes()
    columns = []
    for number in range(7):
        direction = zone_list[number]
        column = np.array(
            [[direction[0] * CX], [direction[1] * CY], [direction[2] * CZ]], np.float32
        )
        columns.append(np.tile(column, (1, block_sizes[number])))
    return jnp.asarray(np.concatenate(columns, axis=1))[:, None, :]


def share_coords(coords, send_list):
    sizes_all = zone_sizes()
    outgoing = split_blocks(jnp.take(coords, send_list, axis=2), sizes_all)
    along_y = from_behind(
        jnp.concatenate([outgoing[1], outgoing[3], outgoing[5], outgoing[6]], axis=2), "gy", -1
    )
    got_y = split_blocks(along_y, [sizes_all[1], sizes_all[3], sizes_all[5], sizes_all[6]])
    along_x = from_behind(
        jnp.concatenate([outgoing[0], outgoing[4], got_y[1], got_y[3]], axis=2), "gx", -1
    )
    got_x = split_blocks(along_x, [sizes_all[0], sizes_all[4], sizes_all[3], sizes_all[6]])
    along_z = from_behind(
        jnp.concatenate([outgoing[2], got_x[1], got_y[2], got_x[3]], axis=2), "gz", -1
    )
    got_z = split_blocks(along_z, [sizes_all[2], sizes_all[4], sizes_all[5], sizes_all[6]])
    received = [got_x[0], got_y[0], got_z[0], got_x[2], got_z[1], got_z[2], got_z[3]]
    return jnp.concatenate(received, axis=2) + shell_offsets()


def return_forces(halo_forces):
    sizes_all = zone_sizes()
    outgoing = split_blocks(halo_forces, sizes_all)
    along_z = from_behind(
        jnp.concatenate([outgoing[2], outgoing[4], outgoing[5], outgoing[6]], axis=2), "gz", 1
    )
    got_z = split_blocks(along_z, [sizes_all[2], sizes_all[4], sizes_all[5], sizes_all[6]])
    along_x = from_behind(
        jnp.concatenate([outgoing[0], outgoing[3], got_z[1], got_z[3]], axis=2), "gx", 1
    )
    got_x = split_blocks(along_x, [sizes_all[0], sizes_all[3], sizes_all[4], sizes_all[6]])
    settled = [got_x[0], got_z[0], got_x[2]]
    pending = [got_x[1], got_z[2], got_x[3]]
    along_y = from_behind(
        jnp.concatenate([outgoing[1], pending[0], pending[1], pending[2]], axis=2), "gy", 1
    )
    got_y = split_blocks(along_y, [sizes_all[1], sizes_all[3], sizes_all[5], sizes_all[6]])
    return jnp.concatenate(
        [settled[0], got_y[0], settled[1], got_y[1], settled[2], got_y[2], got_y[3]], axis=2
    )


def pair_tables(pair_list, extended_count):
    rows = lax.broadcasted_iota(jnp.int32, (extended_count, pair_list.shape[1]), 0)
    first_table = (rows == pair_list[0][None, :]).astype(jnp.float32)
    second_table = (rows == pair_list[1][None, :]).astype(jnp.float32)
    return (first_table, second_table)


def domain_forces(extended, pair_list, tables):
    extended_count = extended.shape[2]
    slot_count = pair_list.shape[1]
    first_ids = pair_list[0]
    second_ids = pair_list[1]
    flat = extended.reshape(24, extended_count)
    first_coords = jnp.dot(flat, tables[0], precision=lax.Precision.HIGHEST).reshape(
        3, 8, slot_count
    )
    second_coords = jnp.dot(flat, tables[1], precision=lax.Precision.HIGHEST).reshape(
        3, 8, slot_count
    )
    separation = first_coords[:, :, None, :] - second_coords[:, None, :, :]
    scaled = jnp.sum(separation * separation, axis=0)
    intersect = jnp.maximum(1.0 - scaled, 0.0)
    bead_row = lax.broadcasted_iota(jnp.int32, (8, 8, 1), 0)
    bead_column = lax.broadcasted_iota(jnp.int32, (8, 8, 1), 1)
    self_pair = (first_ids == second_ids)[None, None, :]
    usable = (first_ids < extended_count - 1)[None, None, :]
    weight = (jnp.where(self_pair, bead_row < bead_column, True) & usable).astype(jnp.float32)
    energy = strength * jnp.sum(weight * intersect * intersect * intersect)
    magnitude = 6.0 * strength * weight * intersect * intersect
    pushing = magnitude[None] * separation
    on_first = jnp.sum(pushing, axis=2).reshape(24, slot_count)
    on_second = (-jnp.sum(pushing, axis=1)).reshape(24, slot_count)
    contract = (((1,), (1,)), ((), ()))
    forces = lax.dot_general(on_first, tables[0], contract, precision=lax.Precision.HIGHEST)
    forces = forces + lax.dot_general(
        on_second, tables[1], contract, precision=lax.Precision.HIGHEST
    )
    return (forces.reshape(3, 8, extended_count), energy)


def local_forces(coords, send_list, pair_list, tables):
    halo_coords = share_coords(coords, send_list)
    dummy_cluster = jnp.zeros((3, 8, 1), jnp.float32)
    extended = jnp.concatenate([coords, halo_coords, dummy_cluster], axis=2)
    forces, energy = domain_forces(extended, pair_list, tables)
    cluster_count = coords.shape[2]
    returned = return_forces(forces[:, :, cluster_count : cluster_count + send_list.shape[0]])
    home_forces = forces[:, :, :cluster_count].at[:, :, send_list].add(returned)
    return (home_forces, energy)


def link_vectors(coords):
    return coords[:, :-1, :] - coords[:, 1:, :]


def link_lengths(coords):
    vectors = link_vectors(coords)
    return jnp.sqrt(jnp.sum(vectors * vectors, axis=0))


def expand(coupling, source):
    coupling_down = jnp.pad(coupling, ((1, 0), (0, 0)))
    coupling_up = jnp.pad(coupling, ((0, 1), (0, 0)))
    series = source
    result = source
    for expansion in range(NORDER):
        series = (
            coupling_down * jnp.pad(series, ((1, 0), (0, 0)))[:-1]
            + coupling_up * jnp.pad(series, ((0, 1), (0, 0)))[1:]
        )
        result = result + series
    return result


def apply_links(coords, directions, solution):
    shifts = directions * (root_half * solution)[None]
    return (
        coords
        - jnp.pad(shifts, ((0, 0), (0, 1), (0, 0)))
        + jnp.pad(shifts, ((0, 0), (1, 0), (0, 0)))
    )


def constrain(previous, updated, rest_length, link_flags):
    old_vectors = link_vectors(previous)
    directions = (
        old_vectors / jnp.maximum(jnp.sqrt(jnp.sum(old_vectors * old_vectors, axis=0)), 0.2)[None]
    )
    coupling = (
        0.5
        * jnp.sum(directions[:, :-1] * directions[:, 1:], axis=0)
        * link_flags[:-1]
        * link_flags[1:]
    )
    projected = jnp.sum(directions * link_vectors(updated), axis=0)
    solution = expand(coupling, link_flags * root_half * (projected - rest_length))
    updated = apply_links(updated, directions, solution)
    vectors = link_vectors(updated)
    squared = jnp.sum(vectors * vectors, axis=0)
    target = jnp.sqrt(
        jnp.maximum(2.0 * rest_length * rest_length - squared, 0.25 * rest_length * rest_length)
    )
    solution = expand(coupling, link_flags * root_half * (rest_length - target))
    updated = apply_links(updated, directions, solution)
    return updated


def on_device(positions, velocities, send_list, pair_list, constraint_flags):
    link_flags = constraint_flags.astype(jnp.float32)
    rest_length = link_lengths(positions)
    bead_total = 8 * positions.shape[2] * lax.axis_size(("gx", "gy", "gz"))
    tables = pair_tables(pair_list, positions.shape[2] + send_list.shape[0] + 1)
    forces, potential = local_forces(positions, send_list, pair_list, tables)
    energy_rows = []
    for iteration in range(ITERS):
        half_speed = velocities + 0.5 * time_step * forces
        updated = constrain(positions, positions + time_step * half_speed, rest_length, link_flags)
        half_speed = (updated - positions) / time_step
        forces, potential = local_forces(updated, send_list, pair_list, tables)
        velocities = half_speed + 0.5 * time_step * forces
        positions = updated
        kinetic = 0.5 * jnp.sum(velocities * velocities)
        energy_rows.append(jnp.stack([potential, kinetic]))
    energies = jnp.stack(energy_rows)
    energies = lax.psum(energies, ("gx", "gy", "gz"))
    return (positions, velocities, energies / bead_total)


def solution(mesh):
    return jax.shard_map(
        on_device,
        mesh=mesh,
        in_specs=(
            P(None, None, ("runs", "gx", "gy", "gz")),
            P(None, None, ("runs", "gx", "gy", "gz")),
            P(("runs", "gx", "gy", "gz")),
            P(None, ("runs", "gx", "gy", "gz")),
            P(None, ("runs", "gx", "gy", "gz")),
        ),
        out_specs=(
            P(None, None, ("runs", "gx", "gy", "gz")),
            P(None, None, ("runs", "gx", "gy", "gz")),
            P("runs", None),
        ),
        check_vma=False,
    )
```

profile of v0, /device:TPU:0, one launch (start us, length us, event | category | flops | bytes accessed | tf_op | source)
XLA Modules:
  0.0 178.5 jit_solution(6793706241259081876)
XLA Ops:
  2.0 0.9 copy.99
  2.9 0.8 gather_fusion
  4.1 3.0 %collective-permute-start = (f32[3,8,34]{2,1,0:T(8,128)S(1)}, f32[3,8,34]{2,1,0:T(8,128)S(1)}, u32[]{:S(2)}, u32[]{:S(2)}) collective-permute-start(f32[3,8,34]{2,1,0:T(8,128)S(1)} %pad_maximum_fusion.8), channel_id=1, source_target_pairs={{0,2},{2,0},{1,3},{3,1},{4,6},{6,4},{5,7},{7,5},{8,10},{10,8},{9,1... | collective-permute-start | bytes 9800 | tf_op jit(solution)/shard_map/ppermute | solution.py:20
  7.2 1.5 collective-permute-done
  9.0 4.1 %collective-permute-start.1 = (f32[3,8,153]{2,1,0:T(8,128)S(1)}, f32[3,8,153]{2,1,0:T(8,128)S(1)}, u32[]{:S(2)}, u32[]{:S(2)}) collective-permute-start(f32[3,8,153]{2,1,0:T(8,128)S(1)} %pad_maximum_fusion), channel_id=1, source_target_pairs={{0,12},{4,0},{8,4},{12,8},{1,13},{5,1},{9,5},{13,9},{2,14},{6,2},{... | collective-permute-start | bytes 44072 | tf_op jit(solution)/shard_map/ppermute | solution.py:20
  13.2 1.5 collective-permute-done.1
  15.0 1.0 collective-permute-done.2
  16.2 0.9 fusion.24
  17.1 0.9 fusion.11
  18.8 1.1 fusion.3
  19.9 1.1 fusion.55
  21.4 1.0 collective-permute-done.3
  23.0 5.6 %collective-permute-done.4 = f32[3,8,153]{2,1,0:T(8,128)S(1)} collective-permute-done((f32[3,8,153]{2,1,0:T(8,128)S(1)}, f32[3,8,153]{2,1,0:T(8,128)S(1)}, u32[]{:S(2)}, u32[]{:S(2)}) %collective-permute-start.4) | collective-permute-done | bytes 14720 | tf_op jit(solution)/shard_map/ppermute | solution.py:20
  28.7 1.5 collective-permute-start.5
  30.5 2.0 %collective-permute-done.5 = f32[3,8,34]{2,1,0:T(8,128)S(1)} collective-permute-done((f32[3,8,34]{2,1,0:T(8,128)S(1)}, f32[3,8,34]{2,1,0:T(8,128)S(1)}, u32[]{:S(2)}, u32[]{:S(2)}) %collective-permute-start.5) | collective-permute-done | bytes 3296 | tf_op jit(solution)/shard_map/ppermute | solution.py:20
  32.9 7.2 %scatter_fusion = f32[3,8,128]{1,0,2:T(4,128)S(1)} fusion(f32[3,8,128]{1,0,2:T(4,128)S(1)} %copy.120, s32[178]{0:T(256)S(1)} %compare_select_fusion, f32[178,3,8]{2,1,0:T(4,128)S(1)} %copy.102), kind=kCustom, calls=%fused_computation.4 | custom fusion | flops 4272 | bytes 51976 | tf_op jit(solution)/shard_map/scatter-add | solution.py:143
  40.6 0.8 gather_fusion.1
  41.9 1.5 collective-permute-start.6
  43.4 2.1 %collective-permute-done.6 = f32[3,8,34]{2,1,0:T(8,128)S(1)} collective-permute-done((f32[3,8,34]{2,1,0:T(8,128)S(1)}, f32[3,8,34]{2,1,0:T(8,128)S(1)}, u32[]{:S(2)}, u32[]{:S(2)}) %collective-permute-start.6) | collective-permute-done | bytes 3296 | tf_op jit(solution)/shard_map/ppermute | solution.py:20
  45.8 2.0 %collective-permute-start.7 = (f32[3,8,153]{2,1,0:T(8,128)S(1)}, f32[3,8,153]{2,1,0:T(8,128)S(1)}, u32[]{:S(2)}, u32[]{:S(2)}) collective-permute-start(f32[3,8,153]{2,1,0:T(8,128)S(1)} %pad_maximum_fusion.2), channel_id=1, source_target_pairs={{0,12},{4,0},{8,4},{12,8},{1,13},{5,1},{9,5},{13,9},{2,14},{6,2},{... | collective-permute-start | bytes 44072 | tf_op jit(solution)/shard_map/ppermute | solution.py:20
  47.8 1.8 %collective-permute-done.7 = f32[3,8,153]{2,1,0:T(8,128)S(1)} collective-permute-done((f32[3,8,153]{2,1,0:T(8,128)S(1)}, f32[3,8,153]{2,1,0:T(8,128)S(1)}, u32[]{:S(2)}, u32[]{:S(2)}) %collective-permute-start.7) | collective-permute-done | bytes 14720 | tf_op jit(solution)/shard_map/ppermute | solution.py:20
  49.9 1.1 collective-permute-done.8
  51.1 0.9 fusion.22
  52.0 0.9 fusion.9
  53.7 1.1 fusion.1
  54.8 1.1 fusion.59
  56.4 1.0 collective-permute-done.9
  57.8 5.6 %collective-permute-done.10 = f32[3,8,153]{2,1,0:T(8,128)S(1)} collective-permute-done((f32[3,8,153]{2,1,0:T(8,128)S(1)}, f32[3,8,153]{2,1,0:T(8,128)S(1)}, u32[]{:S(2)}, u32[]{:S(2)}) %collective-permute-start.10) | collective-permute-done | bytes 14720 | tf_op jit(solution)/shard_map/ppermute | solution.py:20
  63.5 1.5 collective-permute-start.11
  65.3 2.0 %collective-permute-done.11 = f32[3,8,34]{2,1,0:T(8,128)S(1)} collective-permute-done((f32[3,8,34]{2,1,0:T(8,128)S(1)}, f32[3,8,34]{2,1,0:T(8,128)S(1)}, u32[]{:S(2)}, u32[]{:S(2)}) %collective-permute-start.11) | collective-permute-done | bytes 3296 | tf_op jit(solution)/shard_map/ppermute | solution.py:20
  67.7 7.2 %scatter_fusion.1 = f32[3,8,128]{1,0,2:T(4,128)S(1)} fusion(f32[3,8,128]{1,0,2:T(4,128)S(1)} %copy.121, s32[178]{0:T(256)S(1)} %compare_select_fusion, f32[178,3,8]{2,1,0:T(4,128)S(1)} %copy.107), kind=kCustom, calls=%fused_computation.5 | custom fusion | flops 4272 | bytes 51976 | tf_op jit(solution)/shard_map/scatter-add | solution.py:143
  75.4 0.8 gather_fusion.2
  76.7 1.5 collective-permute-start.12
  78.3 2.1 %collective-permute-done.12 = f32[3,8,34]{2,1,0:T(8,128)S(1)} collective-permute-done((f32[3,8,34]{2,1,0:T(8,128)S(1)}, f32[3,8,34]{2,1,0:T(8,128)S(1)}, u32[]{:S(2)}, u32[]{:S(2)}) %collective-permute-start.12) | collective-permute-done | bytes 3296 | tf_op jit(solution)/shard_map/ppermute | solution.py:20
  80.6 2.0 %collective-permute-start.13 = (f32[3,8,153]{2,1,0:T(8,128)S(1)}, f32[3,8,153]{2,1,0:T(8,128)S(1)}, u32[]{:S(2)}, u32[]{:S(2)}) collective-permute-start(f32[3,8,153]{2,1,0:T(8,128)S(1)} %pad_maximum_fusion.4), channel_id=1, source_target_pairs={{0,12},{4,0},{8,4},{12,8},{1,13},{5,1},{9,5},{13,9},{2,14},{6,2},{... | collective-permute-start | bytes 44072 | tf_op jit(solution)/shard_map/ppermute | solution.py:20
  82.7 1.8 %collective-permute-done.13 = f32[3,8,153]{2,1,0:T(8,128)S(1)} collective-permute-done((f32[3,8,153]{2,1,0:T(8,128)S(1)}, f32[3,8,153]{2,1,0:T(8,128)S(1)}, u32[]{:S(2)}, u32[]{:S(2)}) %collective-permute-start.13) | collective-permute-done | bytes 14720 | tf_op jit(solution)/shard_map/ppermute | solution.py:20
  84.7 1.1 collective-permute-done.14
  86.0 0.9 fusion.20
  86.8 0.9 fusion.7
  88.5 1.1 fusion
  89.6 1.1 fusion.61
  91.2 1.0 collective-permute-done.15
  92.4 5.6 %collective-permute-done.16 = f32[3,8,153]{2,1,0:T(8,128)S(1)} collective-permute-done((f32[3,8,153]{2,1,0:T(8,128)S(1)}, f32[3,8,153]{2,1,0:T(8,128)S(1)}, u32[]{:S(2)}, u32[]{:S(2)}) %collective-permute-start.16) | collective-permute-done | bytes 14720 | tf_op jit(solution)/shard_map/ppermute | solution.py:20
  98.2 1.5 collective-permute-start.17
  99.9 2.0 %collective-permute-done.17 = f32[3,8,34]{2,1,0:T(8,128)S(1)} collective-permute-done((f32[3,8,34]{2,1,0:T(8,128)S(1)}, f32[3,8,34]{2,1,0:T(8,128)S(1)}, u32[]{:S(2)}, u32[]{:S(2)}) %collective-permute-start.17) | collective-permute-done | bytes 3296 | tf_op jit(solution)/shard_map/ppermute | solution.py:20
  102.4 7.2 %scatter_fusion.2 = f32[3,8,128]{1,0,2:T(4,128)S(1)} fusion(f32[3,8,128]{1,0,2:T(4,128)S(1)} %copy.122, s32[178]{0:T(256)S(1)} %compare_select_fusion, f32[178,3,8]{2,1,0:T(4,128)S(1)} %copy.112), kind=kCustom, calls=%fused_computation.6 | custom fusion | flops 4272 | bytes 51976 | tf_op jit(solution)/shard_map/scatter-add | solution.py:143
  110.7 0.8 gather_fusion.3
  111.9 1.5 collective-permute-start.18
  113.5 2.1 %collective-permute-done.18 = f32[3,8,34]{2,1,0:T(8,128)S(1)} collective-permute-done((f32[3,8,34]{2,1,0:T(8,128)S(1)}, f32[3,8,34]{2,1,0:T(8,128)S(1)}, u32[]{:S(2)}, u32[]{:S(2)}) %collective-permute-start.18) | collective-permute-done | bytes 3296 | tf_op jit(solution)/shard_map/ppermute | solution.py:20
  115.9 2.2 %collective-permute-start.19 = (f32[3,8,153]{2,1,0:T(8,128)S(1)}, f32[3,8,153]{2,1,0:T(8,128)S(1)}, u32[]{:S(2)}, u32[]{:S(2)}) collective-permute-start(f32[3,8,153]{2,1,0:T(8,128)S(1)} %pad_maximum_fusion.6), channel_id=1, source_target_pairs={{0,12},{4,0},{8,4},{12,8},{1,13},{5,1},{9,5},{13,9},{2,14},{6,2},{... | collective-permute-start | bytes 44072 | tf_op jit(solution)/shard_map/ppermute | solution.py:20
  118.1 1.8 %collective-permute-done.19 = f32[3,8,153]{2,1,0:T(8,128)S(1)} collective-permute-done((f32[3,8,153]{2,1,0:T(8,128)S(1)}, f32[3,8,153]{2,1,0:T(8,128)S(1)}, u32[]{:S(2)}, u32[]{:S(2)}) %collective-permute-start.19) | collective-permute-done | bytes 14720 | tf_op jit(solution)/shard_map/ppermute | solution.py:20
  120.2 1.1 collective-permute-done.20
  121.4 0.9 fusion.18
  122.3 0.9 fusion.5
  123.3 1.1 fusion.66
  124.9 1.1 fusion.2
  125.9 1.1 fusion.57
  127.5 1.0 collective-permute-done.21
  131.3 3.1 %collective-permute-done.22 = f32[3,8,153]{2,1,0:T(8,128)S(1)} collective-permute-done((f32[3,8,153]{2,1,0:T(8,128)S(1)}, f32[3,8,153]{2,1,0:T(8,128)S(1)}, u32[]{:S(2)}, u32[]{:S(2)}) %collective-permute-start.22) | collective-permute-done | bytes 14720 | tf_op jit(solution)/shard_map/ppermute | solution.py:20
  134.5 1.5 collective-permute-start.23
  137.0 1.2 collective-permute-done.23
  138.7 7.2 %scatter_fusion.3 = f32[3,8,128]{1,0,2:T(4,128)S(1)} fusion(f32[3,8,128]{1,0,2:T(4,128)S(1)} %copy.123, s32[178]{0:T(256)S(1)} %compare_select_fusion, f32[178,3,8]{2,1,0:T(4,128)S(1)} %copy.117), kind=kCustom, calls=%fused_computation.7 | custom fusion | flops 4272 | bytes 51976 | tf_op jit(solution)/shard_map/scatter-add | solution.py:143
  146.0 1.2 multiply_reduce_fusion
  147.9 29.9 %psum.7 = f32[3,2]{1,0:T(4,128)S(1)} all-reduce(f32[3,2]{1,0:T(4,128)S(1)} %pad_maximum_fusion.24), channel_id=1, replica_groups=mesh['runs'=2,'gx'=4,'gy'=2,'gz'=2] {'gx','gy','gz'}, use_global_device_ids=true, to_apply=%region_34.36 | all-reduce | flops 6 | bytes 48 | tf_op jit(solution)/shard_map/psum | solution.py:220
  (262 shorter events, 18.4 us)
Async XLA Ops:
  2.0 5.2 %copy-start.4 = (s32[2,1792]{1,0:T(2,128)S(1)}, s32[2,1792]{1,0:T(2,128)}, u32[]{:S(2)}) copy-start(s32[2,1792]{1,0:T(2,128)} %param.14) | copy-start | bytes 43012
  3.9 12.3 %copy-start.3 = (f32[3,178]{1,0:T(4,128)S(1)}, f32[3,178]{1,0:T(4,128)}, u32[]{:S(2)}) copy-start(f32[3,178]{1,0:T(4,128)} %constant.57.clone) | copy-start | bytes 6412
  3.9 12.3 %copy-start = (f32[3,8,128]{2,1,0:T(8,128)S(1)}, f32[3,8,128]{2,1,0:T(8,128)}, u32[]{:S(2)}) copy-start(f32[3,8,128]{2,1,0:T(8,128)} %param.11) | copy-start | bytes 36868
  4.1 4.6 %collective-permute-start = (f32[3,8,34]{2,1,0:T(8,128)S(1)}, f32[3,8,34]{2,1,0:T(8,128)S(1)}, u32[]{:S(2)}, u32[]{:S(2)}) collective-permute-start(f32[3,8,34]{2,1,0:T(8,128)S(1)} %pad_maximum_fusion.8), channel_id=1, source_target_pairs={{0,2},{2,0},{1,3},{3,1},{4,6},{6,4},{5,7},{7,5},{8,10},{10,8},{9,1... | collective-permute-start | bytes 9800 | tf_op jit(solution)/shard_map/ppermute | solution.py:20
  9.0 5.7 %collective-permute-start.1 = (f32[3,8,153]{2,1,0:T(8,128)S(1)}, f32[3,8,153]{2,1,0:T(8,128)S(1)}, u32[]{:S(2)}, u32[]{:S(2)}) collective-permute-start(f32[3,8,153]{2,1,0:T(8,128)S(1)} %pad_maximum_fusion), channel_id=1, source_target_pairs={{0,12},{4,0},{8,4},{12,8},{1,13},{5,1},{9,5},{13,9},{2,14},{6,2},{... | collective-permute-start | bytes 44072 | tf_op jit(solution)/shard_map/ppermute | solution.py:20
  14.8 1.2 collective-permute-start.2
  19.8 10.4 %copy-start.1 = (s32[7,128]{1,0:T(8,128)S(1)}, s32[7,128]{1,0:T(8,128)}, u32[]{:S(2)}) copy-start(s32[7,128]{1,0:T(8,128)} %param.15) | copy-start | bytes 10756
  21.2 1.2 collective-permute-start.3
  22.7 5.9 %collective-permute-start.4 = (f32[3,8,153]{2,1,0:T(8,128)S(1)}, f32[3,8,153]{2,1,0:T(8,128)S(1)}, u32[]{:S(2)}, u32[]{:S(2)}) collective-permute-start(f32[3,8,153]{2,1,0:T(8,128)S(1)} %pad_maximum_fusion.1), channel_id=1, source_target_pairs={{0,4},{4,8},{8,12},{12,0},{1,5},{5,9},{9,13},{13,1},{2,6},{6,10},{... | collective-permute-start | bytes 44072 | tf_op jit(solution)/shard_map/ppermute | solution.py:20
  28.7 3.7 %collective-permute-start.5 = (f32[3,8,34]{2,1,0:T(8,128)S(1)}, f32[3,8,34]{2,1,0:T(8,128)S(1)}, u32[]{:S(2)}, u32[]{:S(2)}) collective-permute-start(f32[3,8,34]{2,1,0:T(8,128)S(1)} %pad_maximum_fusion.11), channel_id=1, source_target_pairs={{0,2},{2,0},{1,3},{3,1},{4,6},{6,4},{5,7},{7,5},{8,10},{10,8},{9,1... | collective-permute-start | bytes 9800 | tf_op jit(solution)/shard_map/ppermute | solution.py:20
  30.5 9.7 %copy-start.5 = (f32[3,8,128]{2,1,0:T(8,128)S(1)}, f32[3,8,128]{2,1,0:T(8,128)}, u32[]{:S(2)}) copy-start(f32[3,8,128]{2,1,0:T(8,128)} %param.12) | copy-start | bytes 36868
  41.9 3.7 %collective-permute-start.6 = (f32[3,8,34]{2,1,0:T(8,128)S(1)}, f32[3,8,34]{2,1,0:T(8,128)S(1)}, u32[]{:S(2)}, u32[]{:S(2)}) collective-permute-start(f32[3,8,34]{2,1,0:T(8,128)S(1)} %pad_maximum_fusion.12), channel_id=1, source_target_pairs={{0,2},{2,0},{1,3},{3,1},{4,6},{6,4},{5,7},{7,5},{8,10},{10,8},{9,1... | collective-permute-start | bytes 9800 | tf_op jit(solution)/shard_map/ppermute | solution.py:20
  45.8 3.8 %collective-permute-start.7 = (f32[3,8,153]{2,1,0:T(8,128)S(1)}, f32[3,8,153]{2,1,0:T(8,128)S(1)}, u32[]{:S(2)}, u32[]{:S(2)}) collective-permute-start(f32[3,8,153]{2,1,0:T(8,128)S(1)} %pad_maximum_fusion.2), channel_id=1, source_target_pairs={{0,12},{4,0},{8,4},{12,8},{1,13},{5,1},{9,5},{13,9},{2,14},{6,2},{... | collective-permute-start | bytes 44072 | tf_op jit(solution)/shard_map/ppermute | solution.py:20
  49.8 1.2 collective-permute-start.8
  56.2 1.2 collective-permute-start.9
  57.6 5.8 %collective-permute-start.10 = (f32[3,8,153]{2,1,0:T(8,128)S(1)}, f32[3,8,153]{2,1,0:T(8,128)S(1)}, u32[]{:S(2)}, u32[]{:S(2)}) collective-permute-start(f32[3,8,153]{2,1,0:T(8,128)S(1)} %pad_maximum_fusion.3), channel_id=1, source_target_pairs={{0,4},{4,8},{8,12},{12,0},{1,5},{5,9},{9,13},{13,1},{2,6},{6,10},{... | collective-permute-start | bytes 44072 | tf_op jit(solution)/shard_map/ppermute | solution.py:20
  63.5 3.7 %collective-permute-start.11 = (f32[3,8,34]{2,1,0:T(8,128)S(1)}, f32[3,8,34]{2,1,0:T(8,128)S(1)}, u32[]{:S(2)}, u32[]{:S(2)}) collective-permute-start(f32[3,8,34]{2,1,0:T(8,128)S(1)} %pad_maximum_fusion.15), channel_id=1, source_target_pairs={{0,2},{2,0},{1,3},{3,1},{4,6},{6,4},{5,7},{7,5},{8,10},{10,8},{9,1... | collective-permute-start | bytes 9800 | tf_op jit(solution)/shard_map/ppermute | solution.py:20
  76.7 3.7 %collective-permute-start.12 = (f32[3,8,34]{2,1,0:T(8,128)S(1)}, f32[3,8,34]{2,1,0:T(8,128)S(1)}, u32[]{:S(2)}, u32[]{:S(2)}) collective-permute-start(f32[3,8,34]{2,1,0:T(8,128)S(1)} %pad_maximum_fusion.16), channel_id=1, source_target_pairs={{0,2},{2,0},{1,3},{3,1},{4,6},{6,4},{5,7},{7,5},{8,10},{10,8},{9,1... | collective-permute-start | bytes 9800 | tf_op jit(solution)/shard_map/ppermute | solution.py:20
  80.6 3.8 %collective-permute-start.13 = (f32[3,8,153]{2,1,0:T(8,128)S(1)}, f32[3,8,153]{2,1,0:T(8,128)S(1)}, u32[]{:S(2)}, u32[]{:S(2)}) collective-permute-start(f32[3,8,153]{2,1,0:T(8,128)S(1)} %pad_maximum_fusion.4), channel_id=1, source_target_pairs={{0,12},{4,0},{8,4},{12,8},{1,13},{5,1},{9,5},{13,9},{2,14},{6,2},{... | collective-permute-start | bytes 44072 | tf_op jit(solution)/shard_map/ppermute | solution.py:20
  84.6 1.2 collective-permute-start.14
  91.0 1.2 collective-permute-start.15
  92.4 5.6 %collective-permute-start.16 = (f32[3,8,153]{2,1,0:T(8,128)S(1)}, f32[3,8,153]{2,1,0:T(8,128)S(1)}, u32[]{:S(2)}, u32[]{:S(2)}) collective-permute-start(f32[3,8,153]{2,1,0:T(8,128)S(1)} %pad_maximum_fusion.5), channel_id=1, source_target_pairs={{0,4},{4,8},{8,12},{12,0},{1,5},{5,9},{9,13},{13,1},{2,6},{6,10},{... | collective-permute-start | bytes 44072 | tf_op jit(solution)/shard_map/ppermute | solution.py:20
  98.2 3.7 %collective-permute-start.17 = (f32[3,8,34]{2,1,0:T(8,128)S(1)}, f32[3,8,34]{2,1,0:T(8,128)S(1)}, u32[]{:S(2)}, u32[]{:S(2)}) collective-permute-start(f32[3,8,34]{2,1,0:T(8,128)S(1)} %pad_maximum_fusion.19), channel_id=1, source_target_pairs={{0,2},{2,0},{1,3},{3,1},{4,6},{6,4},{5,7},{7,5},{8,10},{10,8},{9,1... | collective-permute-start | bytes 9800 | tf_op jit(solution)/shard_map/ppermute | solution.py:20
  110.5 35.4 %copy-start.2 = (f32[3,8,128]{2,1,0:T(8,128)}, f32[3,8,128]{2,1,0:T(8,128)S(1)}, u32[]{:S(2)}) copy-start(f32[3,8,128]{2,1,0:T(8,128)S(1)} %pad_add_fusion) | copy-start | bytes 36868
  111.9 3.7 %collective-permute-start.18 = (f32[3,8,34]{2,1,0:T(8,128)S(1)}, f32[3,8,34]{2,1,0:T(8,128)S(1)}, u32[]{:S(2)}, u32[]{:S(2)}) collective-permute-start(f32[3,8,34]{2,1,0:T(8,128)S(1)} %pad_maximum_fusion.20), channel_id=1, source_target_pairs={{0,2},{2,0},{1,3},{3,1},{4,6},{6,4},{5,7},{7,5},{8,10},{10,8},{9,1... | collective-permute-start | bytes 9800 | tf_op jit(solution)/shard_map/ppermute | solution.py:20
  115.9 4.0 %collective-permute-start.19 = (f32[3,8,153]{2,1,0:T(8,128)S(1)}, f32[3,8,153]{2,1,0:T(8,128)S(1)}, u32[]{:S(2)}, u32[]{:S(2)}) collective-permute-start(f32[3,8,153]{2,1,0:T(8,128)S(1)} %pad_maximum_fusion.6), channel_id=1, source_target_pairs={{0,12},{4,0},{8,4},{12,8},{1,13},{5,1},{9,5},{13,9},{2,14},{6,2},{... | collective-permute-start | bytes 44072 | tf_op jit(solution)/shard_map/ppermute | solution.py:20
  120.1 1.2 collective-permute-start.20
  127.3 1.2 collective-permute-start.21
  128.8 5.6 %collective-permute-start.22 = (f32[3,8,153]{2,1,0:T(8,128)S(1)}, f32[3,8,153]{2,1,0:T(8,128)S(1)}, u32[]{:S(2)}, u32[]{:S(2)}) collective-permute-start(f32[3,8,153]{2,1,0:T(8,128)S(1)} %pad_maximum_fusion.7), channel_id=1, source_target_pairs={{0,4},{4,8},{8,12},{12,0},{1,5},{5,9},{9,13},{13,1},{2,6},{6,10},{... | collective-permute-start | bytes 44072 | tf_op jit(solution)/shard_map/ppermute | solution.py:20
  134.5 3.7 %collective-permute-start.23 = (f32[3,8,34]{2,1,0:T(8,128)S(1)}, f32[3,8,34]{2,1,0:T(8,128)S(1)}, u32[]{:S(2)}, u32[]{:S(2)}) collective-permute-start(f32[3,8,34]{2,1,0:T(8,128)S(1)} %pad_maximum_fusion.23), channel_id=1, source_target_pairs={{0,2},{2,0},{1,3},{3,1},{4,6},{6,4},{5,7},{7,5},{8,10},{10,8},{9,1... | collective-permute-start | bytes 9800 | tf_op jit(solution)/shard_map/ppermute | solution.py:20
where the time goes:
time: 179 us
  waiting for transfers between devices  50.2 us (28%)
  other arithmetic  38.8 us (22%)
  blocking collectives  29.9 us (17%)
  starting transfers between devices  25.1 us (14%)
  matrix products  15.5 us (9%)
  local copies, waits for them, and re-layouts  13.6 us (8%)
  between operations  5.39 us (3%)
    ppermute x24, waiting for transfers between devices, from_behind(): lax.ppermute(value, axis, [(i, (i + by) % count) for i in range(count)])  50.2 us
    psum x1, blocking collectives, on_device(): energies = lax.psum(energies, ('gx', 'gy', 'gz'))  29.9 us
    scatter-add x4, other arithmetic, local_forces(): home_forces = forces[:, :, :cluster_count].at[:, :, send_list].add(returned)  28.6 us
    ppermute x24, starting transfers between devices, from_behind(): lax.ppermute(value, axis, [(i, (i + by) % count) for i in range(count)])  25.1 us
    slice x92, local copies, waits for them, and re-layouts, split_blocks(): pieces.append(packed[:, :, position:position + length])  4.99 us
    dot_general x4, matrix products, domain_forces(): lax.dot_general(on_first, tables[0], contract, precision=lax.Precision.HI...  4.36 us
    dot_general x4, matrix products, domain_forces(): lax.dot_general(on_second, tables[1], contract, precision=lax.Precision.H...  4.27 us
    gather x8, local copies, waits for them, and re-layouts, share_coords(): outgoing = split_blocks(jnp.take(coords, send_list, axis=2), sizes_all)  3.98 us
  transfers between devices with their start and end apart: 24, of which 24 were waited for; matrix products, arithmetic and copies ran while one was open for 1% of the time, Pallas kernels for 0%

commit v1 on v0

--- a/solution.py
+++ b/solution.py
@@ -217,7 +217,7 @@
         kinetic = 0.5 * jnp.sum(velocities * velocities)
         energy_rows.append(jnp.stack([potential, kinetic]))
     energies = jnp.stack(energy_rows)
-    energies = lax.psum(energies, ("gx", "gy", "gz"))
+    energies = jnp.sum(lax.all_gather(energies, ("gx", "gy", "gz")), axis=0)
     return (positions, velocities, energies / bead_total)
 
 

time: 179 us -> 169 us (0.944)
  blocking collectives: 29.9 us -> 20 us
    psum x1 -> x0, blocking collectives: 29.9 us -> none  [on_device(): energies = lax.psum(energies, ('gx', 'gy', 'gz'))]
    all_gather x0 -> x1, blocking collectives: none -> 20 us  [on_device(): energies = jnp.sum(lax.all_gather(energies, ('gx', 'gy', 'gz')), axis=0)]
where the time goes in v1:
time: 169 us
  waiting for transfers between devices  50.2 us (30%)
  other arithmetic  39.4 us (23%)
  starting transfers between devices  25.1 us (15%)
  blocking collectives  20 us (12%)
  matrix products  15.5 us (9%)
  local copies, waits for them, and re-layouts  13 us (8%)
  between operations  5.39 us (3%)
    ppermute x24, waiting for transfers between devices, from_behind(): lax.ppermute(value, axis, [(i, (i + by) % count) for i in range(count)])  50.2 us
    scatter-add x4, other arithmetic, local_forces(): home_forces = forces[:, :, :cluster_count].at[:, :, send_list].add(returned)  28.6 us
    ppermute x24, starting transfers between devices, from_behind(): lax.ppermute(value, axis, [(i, (i + by) % count) for i in range(count)])  25.1 us
    all_gather x1, blocking collectives, on_device(): energies = jnp.sum(lax.all_gather(energies, ('gx', 'gy', 'gz')), axis=0)  20 us
    slice x92, local copies, waits for them, and re-layouts, split_blocks(): pieces.append(packed[:, :, position:position + length])  4.99 us
    dot_general x4, matrix products, domain_forces(): lax.dot_general(on_first, tables[0], contract, precision=lax.Precision.HI...  4.36 us
    dot_general x4, matrix products, domain_forces(): lax.dot_general(on_second, tables[1], contract, precision=lax.Precision.H...  4.27 us
    gather x8, local copies, waits for them, and re-layouts, share_coords(): outgoing = split_blocks(jnp.take(coords, send_list, axis=2), sizes_all)  3.98 us
  transfers between devices with their start and end apart: 24, of which 24 were waited for; matrix products, arithmetic and copies ran while one was open for 1% of the time, Pallas kernels for 0%

profile of v1, /device:TPU:0, one launch (start us, length us, event | category | flops | bytes accessed | tf_op | source)
XLA Modules:
  0.0 168.7 jit_solution(3047174580836648677)
XLA Ops:
  2.0 0.9 copy.99
  2.9 0.8 gather_fusion
  4.1 3.0 %collective-permute-start = (f32[3,8,34]{2,1,0:T(8,128)S(1)}, f32[3,8,34]{2,1,0:T(8,128)S(1)}, u32[]{:S(2)}, u32[]{:S(2)}) collective-permute-start(f32[3,8,34]{2,1,0:T(8,128)S(1)} %pad_maximum_fusion.8), channel_id=1, source_target_pairs={{0,2},{2,0},{1,3},{3,1},{4,6},{6,4},{5,7},{7,5},{8,10},{10,8},{9,1... | collective-permute-start | bytes 9800 | tf_op jit(solution)/shard_map/ppermute | solution.py:20
  7.2 1.5 collective-permute-done
  9.0 4.1 %collective-permute-start.1 = (f32[3,8,153]{2,1,0:T(8,128)S(1)}, f32[3,8,153]{2,1,0:T(8,128)S(1)}, u32[]{:S(2)}, u32[]{:S(2)}) collective-permute-start(f32[3,8,153]{2,1,0:T(8,128)S(1)} %pad_maximum_fusion), channel_id=1, source_target_pairs={{0,12},{4,0},{8,4},{12,8},{1,13},{5,1},{9,5},{13,9},{2,14},{6,2},{... | collective-permute-start | bytes 44072 | tf_op jit(solution)/shard_map/ppermute | solution.py:20
  13.2 1.5 collective-permute-done.1
  15.0 1.0 collective-permute-done.2
  16.2 0.9 fusion.24
  17.1 0.9 fusion.11
  18.8 1.1 fusion.3
  19.9 1.1 fusion.55
  21.4 1.0 collective-permute-done.3
  22.9 5.6 %collective-permute-done.4 = f32[3,8,153]{2,1,0:T(8,128)S(1)} collective-permute-done((f32[3,8,153]{2,1,0:T(8,128)S(1)}, f32[3,8,153]{2,1,0:T(8,128)S(1)}, u32[]{:S(2)}, u32[]{:S(2)}) %collective-permute-start.4) | collective-permute-done | bytes 14720 | tf_op jit(solution)/shard_map/ppermute | solution.py:20
  28.7 1.5 collective-permute-start.5
  30.5 2.0 %collective-permute-done.5 = f32[3,8,34]{2,1,0:T(8,128)S(1)} collective-permute-done((f32[3,8,34]{2,1,0:T(8,128)S(1)}, f32[3,8,34]{2,1,0:T(8,128)S(1)}, u32[]{:S(2)}, u32[]{:S(2)}) %collective-permute-start.5) | collective-permute-done | bytes 3296 | tf_op jit(solution)/shard_map/ppermute | solution.py:20
  32.9 7.2 %scatter_fusion = f32[3,8,128]{1,0,2:T(4,128)S(1)} fusion(f32[3,8,128]{1,0,2:T(4,128)S(1)} %copy.120, s32[178]{0:T(256)S(1)} %compare_select_fusion, f32[178,3,8]{2,1,0:T(4,128)S(1)} %copy.102), kind=kCustom, calls=%fused_computation.4 | custom fusion | flops 4272 | bytes 51976 | tf_op jit(solution)/shard_map/scatter-add | solution.py:143
  40.6 0.8 gather_fusion.1
  41.9 1.5 collective-permute-start.6
  43.4 2.1 %collective-permute-done.6 = f32[3,8,34]{2,1,0:T(8,128)S(1)} collective-permute-done((f32[3,8,34]{2,1,0:T(8,128)S(1)}, f32[3,8,34]{2,1,0:T(8,128)S(1)}, u32[]{:S(2)}, u32[]{:S(2)}) %collective-permute-start.6) | collective-permute-done | bytes 3296 | tf_op jit(solution)/shard_map/ppermute | solution.py:20
  45.8 2.0 %collective-permute-start.7 = (f32[3,8,153]{2,1,0:T(8,128)S(1)}, f32[3,8,153]{2,1,0:T(8,128)S(1)}, u32[]{:S(2)}, u32[]{:S(2)}) collective-permute-start(f32[3,8,153]{2,1,0:T(8,128)S(1)} %pad_maximum_fusion.2), channel_id=1, source_target_pairs={{0,12},{4,0},{8,4},{12,8},{1,13},{5,1},{9,5},{13,9},{2,14},{6,2},{... | collective-permute-start | bytes 44072 | tf_op jit(solution)/shard_map/ppermute | solution.py:20
  47.8 1.8 %collective-permute-done.7 = f32[3,8,153]{2,1,0:T(8,128)S(1)} collective-permute-done((f32[3,8,153]{2,1,0:T(8,128)S(1)}, f32[3,8,153]{2,1,0:T(8,128)S(1)}, u32[]{:S(2)}, u32[]{:S(2)}) %collective-permute-start.7) | collective-permute-done | bytes 14720 | tf_op jit(solution)/shard_map/ppermute | solution.py:20
  49.9 1.1 collective-permute-done.8
  51.1 0.9 fusion.22
  52.0 0.9 fusion.9
  53.7 1.1 fusion.1
  54.8 1.1 fusion.59
  56.4 1.0 collective-permute-done.9
  57.8 5.6 %collective-permute-done.10 = f32[3,8,153]{2,1,0:T(8,128)S(1)} collective-permute-done((f32[3,8,153]{2,1,0:T(8,128)S(1)}, f32[3,8,153]{2,1,0:T(8,128)S(1)}, u32[]{:S(2)}, u32[]{:S(2)}) %collective-permute-start.10) | collective-permute-done | bytes 14720 | tf_op jit(solution)/shard_map/ppermute | solution.py:20
  63.5 1.5 collective-permute-start.11
  65.3 2.0 %collective-permute-done.11 = f32[3,8,34]{2,1,0:T(8,128)S(1)} collective-permute-done((f32[3,8,34]{2,1,0:T(8,128)S(1)}, f32[3,8,34]{2,1,0:T(8,128)S(1)}, u32[]{:S(2)}, u32[]{:S(2)}) %collective-permute-start.11) | collective-permute-done | bytes 3296 | tf_op jit(solution)/shard_map/ppermute | solution.py:20
  67.7 7.2 %scatter_fusion.1 = f32[3,8,128]{1,0,2:T(4,128)S(1)} fusion(f32[3,8,128]{1,0,2:T(4,128)S(1)} %copy.121, s32[178]{0:T(256)S(1)} %compare_select_fusion, f32[178,3,8]{2,1,0:T(4,128)S(1)} %copy.107), kind=kCustom, calls=%fused_computation.5 | custom fusion | flops 4272 | bytes 51976 | tf_op jit(solution)/shard_map/scatter-add | solution.py:143
  75.4 0.8 gather_fusion.2
  76.7 1.5 collective-permute-start.12
  78.3 2.1 %collective-permute-done.12 = f32[3,8,34]{2,1,0:T(8,128)S(1)} collective-permute-done((f32[3,8,34]{2,1,0:T(8,128)S(1)}, f32[3,8,34]{2,1,0:T(8,128)S(1)}, u32[]{:S(2)}, u32[]{:S(2)}) %collective-permute-start.12) | collective-permute-done | bytes 3296 | tf_op jit(solution)/shard_map/ppermute | solution.py:20
  80.6 2.0 %collective-permute-start.13 = (f32[3,8,153]{2,1,0:T(8,128)S(1)}, f32[3,8,153]{2,1,0:T(8,128)S(1)}, u32[]{:S(2)}, u32[]{:S(2)}) collective-permute-start(f32[3,8,153]{2,1,0:T(8,128)S(1)} %pad_maximum_fusion.4), channel_id=1, source_target_pairs={{0,12},{4,0},{8,4},{12,8},{1,13},{5,1},{9,5},{13,9},{2,14},{6,2},{... | collective-permute-start | bytes 44072 | tf_op jit(solution)/shard_map/ppermute | solution.py:20
  82.7 1.8 %collective-permute-done.13 = f32[3,8,153]{2,1,0:T(8,128)S(1)} collective-permute-done((f32[3,8,153]{2,1,0:T(8,128)S(1)}, f32[3,8,153]{2,1,0:T(8,128)S(1)}, u32[]{:S(2)}, u32[]{:S(2)}) %collective-permute-start.13) | collective-permute-done | bytes 14720 | tf_op jit(solution)/shard_map/ppermute | solution.py:20
  84.7 1.1 collective-permute-done.14
  86.0 0.9 fusion.20
  86.8 0.9 fusion.7
  88.5 1.1 fusion
  89.6 1.1 fusion.61
  91.2 1.0 collective-permute-done.15
  92.4 5.6 %collective-permute-done.16 = f32[3,8,153]{2,1,0:T(8,128)S(1)} collective-permute-done((f32[3,8,153]{2,1,0:T(8,128)S(1)}, f32[3,8,153]{2,1,0:T(8,128)S(1)}, u32[]{:S(2)}, u32[]{:S(2)}) %collective-permute-start.16) | collective-permute-done | bytes 14720 | tf_op jit(solution)/shard_map/ppermute | solution.py:20
  98.2 1.5 collective-permute-start.17
  99.9 2.0 %collective-permute-done.17 = f32[3,8,34]{2,1,0:T(8,128)S(1)} collective-permute-done((f32[3,8,34]{2,1,0:T(8,128)S(1)}, f32[3,8,34]{2,1,0:T(8,128)S(1)}, u32[]{:S(2)}, u32[]{:S(2)}) %collective-permute-start.17) | collective-permute-done | bytes 3296 | tf_op jit(solution)/shard_map/ppermute | solution.py:20
  102.4 7.2 %scatter_fusion.2 = f32[3,8,128]{1,0,2:T(4,128)S(1)} fusion(f32[3,8,128]{1,0,2:T(4,128)S(1)} %copy.122, s32[178]{0:T(256)S(1)} %compare_select_fusion, f32[178,3,8]{2,1,0:T(4,128)S(1)} %copy.112), kind=kCustom, calls=%fused_computation.6 | custom fusion | flops 4272 | bytes 51976 | tf_op jit(solution)/shard_map/scatter-add | solution.py:143
  110.7 0.8 gather_fusion.3
  111.9 1.5 collective-permute-start.18
  113.5 2.1 %collective-permute-done.18 = f32[3,8,34]{2,1,0:T(8,128)S(1)} collective-permute-done((f32[3,8,34]{2,1,0:T(8,128)S(1)}, f32[3,8,34]{2,1,0:T(8,128)S(1)}, u32[]{:S(2)}, u32[]{:S(2)}) %collective-permute-start.18) | collective-permute-done | bytes 3296 | tf_op jit(solution)/shard_map/ppermute | solution.py:20
  115.9 2.2 %collective-permute-start.19 = (f32[3,8,153]{2,1,0:T(8,128)S(1)}, f32[3,8,153]{2,1,0:T(8,128)S(1)}, u32[]{:S(2)}, u32[]{:S(2)}) collective-permute-start(f32[3,8,153]{2,1,0:T(8,128)S(1)} %pad_maximum_fusion.6), channel_id=1, source_target_pairs={{0,12},{4,0},{8,4},{12,8},{1,13},{5,1},{9,5},{13,9},{2,14},{6,2},{... | collective-permute-start | bytes 44072 | tf_op jit(solution)/shard_map/ppermute | solution.py:20
  118.1 1.8 %collective-permute-done.19 = f32[3,8,153]{2,1,0:T(8,128)S(1)} collective-permute-done((f32[3,8,153]{2,1,0:T(8,128)S(1)}, f32[3,8,153]{2,1,0:T(8,128)S(1)}, u32[]{:S(2)}, u32[]{:S(2)}) %collective-permute-start.19) | collective-permute-done | bytes 14720 | tf_op jit(solution)/shard_map/ppermute | solution.py:20
  120.2 1.1 collective-permute-done.20
  121.4 0.9 fusion.18
  122.3 0.9 fusion.5
  123.3 1.1 fusion.66
  124.9 1.1 fusion.2
  125.9 1.1 fusion.57
  127.5 1.0 collective-permute-done.21
  131.3 3.1 %collective-permute-done.22 = f32[3,8,153]{2,1,0:T(8,128)S(1)} collective-permute-done((f32[3,8,153]{2,1,0:T(8,128)S(1)}, f32[3,8,153]{2,1,0:T(8,128)S(1)}, u32[]{:S(2)}, u32[]{:S(2)}) %collective-permute-start.22) | collective-permute-done | bytes 14720 | tf_op jit(solution)/shard_map/ppermute | solution.py:20
  134.5 1.5 collective-permute-start.23
  137.0 1.2 collective-permute-done.23
  138.7 7.2 %scatter_fusion.3 = f32[3,8,128]{1,0,2:T(4,128)S(1)} fusion(f32[3,8,128]{1,0,2:T(4,128)S(1)} %copy.123, s32[178]{0:T(256)S(1)} %compare_select_fusion, f32[178,3,8]{2,1,0:T(4,128)S(1)} %copy.117), kind=kCustom, calls=%fused_computation.7 | custom fusion | flops 4272 | bytes 51976 | tf_op jit(solution)/shard_map/scatter-add | solution.py:143
  146.0 1.2 multiply_reduce_fusion
  148.0 20.0 %all-gather.1 = f32[16,3,2]{1,2,0:T(2,128)S(1)} all-gather(f32[1,3,2]{1,2,0:T(2,128)S(1)} %bitcast.82), channel_id=2, replica_groups=mesh['runs'=2,'gx'=4,'gy'=2,'gz'=2] {'gx','gy','gz'}, dimensions={0}, use_global_device_ids=true | all-gather | bytes 408 | tf_op jit(solution)/shard_map/all_gather | solution.py:220
  (263 shorter events, 18.4 us)
Async XLA Ops:
  2.0 5.2 %copy-start.4 = (s32[2,1792]{1,0:T(2,128)S(1)}, s32[2,1792]{1,0:T(2,128)}, u32[]{:S(2)}) copy-start(s32[2,1792]{1,0:T(2,128)} %param.14) | copy-start | bytes 43012
  3.9 12.3 %copy-start.3 = (f32[3,178]{1,0:T(4,128)S(1)}, f32[3,178]{1,0:T(4,128)}, u32[]{:S(2)}) copy-start(f32[3,178]{1,0:T(4,128)} %constant.57.clone) | copy-start | bytes 6412
  3.9 12.3 %copy-start = (f32[3,8,128]{2,1,0:T(8,128)S(1)}, f32[3,8,128]{2,1,0:T(8,128)}, u32[]{:S(2)}) copy-start(f32[3,8,128]{2,1,0:T(8,128)} %param.11) | copy-start | bytes 36868
  4.1 4.6 %collective-permute-start = (f32[3,8,34]{2,1,0:T(8,128)S(1)}, f32[3,8,34]{2,1,0:T(8,128)S(1)}, u32[]{:S(2)}, u32[]{:S(2)}) collective-permute-start(f32[3,8,34]{2,1,0:T(8,128)S(1)} %pad_maximum_fusion.8), channel_id=1, source_target_pairs={{0,2},{2,0},{1,3},{3,1},{4,6},{6,4},{5,7},{7,5},{8,10},{10,8},{9,1... | collective-permute-start | bytes 9800 | tf_op jit(solution)/shard_map/ppermute | solution.py:20
  9.0 5.7 %collective-permute-start.1 = (f32[3,8,153]{2,1,0:T(8,128)S(1)}, f32[3,8,153]{2,1,0:T(8,128)S(1)}, u32[]{:S(2)}, u32[]{:S(2)}) collective-permute-start(f32[3,8,153]{2,1,0:T(8,128)S(1)} %pad_maximum_fusion), channel_id=1, source_target_pairs={{0,12},{4,0},{8,4},{12,8},{1,13},{5,1},{9,5},{13,9},{2,14},{6,2},{... | collective-permute-start | bytes 44072 | tf_op jit(solution)/shard_map/ppermute | solution.py:20
  14.8 1.2 collective-permute-start.2
  19.8 10.4 %copy-start.1 = (s32[7,128]{1,0:T(8,128)S(1)}, s32[7,128]{1,0:T(8,128)}, u32[]{:S(2)}) copy-start(s32[7,128]{1,0:T(8,128)} %param.15) | copy-start | bytes 10756
  21.2 1.2 collective-permute-start.3
  22.7 5.9 %collective-permute-start.4 = (f32[3,8,153]{2,1,0:T(8,128)S(1)}, f32[3,8,153]{2,1,0:T(8,128)S(1)}, u32[]{:S(2)}, u32[]{:S(2)}) collective-permute-start(f32[3,8,153]{2,1,0:T(8,128)S(1)} %pad_maximum_fusion.1), channel_id=1, source_target_pairs={{0,4},{4,8},{8,12},{12,0},{1,5},{5,9},{9,13},{13,1},{2,6},{6,10},{... | collective-permute-start | bytes 44072 | tf_op jit(solution)/shard_map/ppermute | solution.py:20
  28.7 3.7 %collective-permute-start.5 = (f32[3,8,34]{2,1,0:T(8,128)S(1)}, f32[3,8,34]{2,1,0:T(8,128)S(1)}, u32[]{:S(2)}, u32[]{:S(2)}) collective-permute-start(f32[3,8,34]{2,1,0:T(8,128)S(1)} %pad_maximum_fusion.11), channel_id=1, source_target_pairs={{0,2},{2,0},{1,3},{3,1},{4,6},{6,4},{5,7},{7,5},{8,10},{10,8},{9,1... | collective-permute-start | bytes 9800 | tf_op jit(solution)/shard_map/ppermute | solution.py:20
  30.5 9.7 %copy-start.5 = (f32[3,8,128]{2,1,0:T(8,128)S(1)}, f32[3,8,128]{2,1,0:T(8,128)}, u32[]{:S(2)}) copy-start(f32[3,8,128]{2,1,0:T(8,128)} %param.12) | copy-start | bytes 36868
  41.9 3.7 %collective-permute-start.6 = (f32[3,8,34]{2,1,0:T(8,128)S(1)}, f32[3,8,34]{2,1,0:T(8,128)S(1)}, u32[]{:S(2)}, u32[]{:S(2)}) collective-permute-start(f32[3,8,34]{2,1,0:T(8,128)S(1)} %pad_maximum_fusion.12), channel_id=1, source_target_pairs={{0,2},{2,0},{1,3},{3,1},{4,6},{6,4},{5,7},{7,5},{8,10},{10,8},{9,1... | collective-permute-start | bytes 9800 | tf_op jit(solution)/shard_map/ppermute | solution.py:20
  45.8 3.8 %collective-permute-start.7 = (f32[3,8,153]{2,1,0:T(8,128)S(1)}, f32[3,8,153]{2,1,0:T(8,128)S(1)}, u32[]{:S(2)}, u32[]{:S(2)}) collective-permute-start(f32[3,8,153]{2,1,0:T(8,128)S(1)} %pad_maximum_fusion.2), channel_id=1, source_target_pairs={{0,12},{4,0},{8,4},{12,8},{1,13},{5,1},{9,5},{13,9},{2,14},{6,2},{... | collective-permute-start | bytes 44072 | tf_op jit(solution)/shard_map/ppermute | solution.py:20
  49.8 1.2 collective-permute-start.8
  56.2 1.2 collective-permute-start.9
  57.6 5.8 %collective-permute-start.10 = (f32[3,8,153]{2,1,0:T(8,128)S(1)}, f32[3,8,153]{2,1,0:T(8,128)S(1)}, u32[]{:S(2)}, u32[]{:S(2)}) collective-permute-start(f32[3,8,153]{2,1,0:T(8,128)S(1)} %pad_maximum_fusion.3), channel_id=1, source_target_pairs={{0,4},{4,8},{8,12},{12,0},{1,5},{5,9},{9,13},{13,1},{2,6},{6,10},{... | collective-permute-start | bytes 44072 | tf_op jit(solution)/shard_map/ppermute | solution.py:20
  63.5 3.7 %collective-permute-start.11 = (f32[3,8,34]{2,1,0:T(8,128)S(1)}, f32[3,8,34]{2,1,0:T(8,128)S(1)}, u32[]{:S(2)}, u32[]{:S(2)}) collective-permute-start(f32[3,8,34]{2,1,0:T(8,128)S(1)} %pad_maximum_fusion.15), channel_id=1, source_target_pairs={{0,2},{2,0},{1,3},{3,1},{4,6},{6,4},{5,7},{7,5},{8,10},{10,8},{9,1... | collective-permute-start | bytes 9800 | tf_op jit(solution)/shard_map/ppermute | solution.py:20
  76.7 3.7 %collective-permute-start.12 = (f32[3,8,34]{2,1,0:T(8,128)S(1)}, f32[3,8,34]{2,1,0:T(8,128)S(1)}, u32[]{:S(2)}, u32[]{:S(2)}) collective-permute-start(f32[3,8,34]{2,1,0:T(8,128)S(1)} %pad_maximum_fusion.16), channel_id=1, source_target_pairs={{0,2},{2,0},{1,3},{3,1},{4,6},{6,4},{5,7},{7,5},{8,10},{10,8},{9,1... | collective-permute-start | bytes 9800 | tf_op jit(solution)/shard_map/ppermute | solution.py:20
  80.6 3.8 %collective-permute-start.13 = (f32[3,8,153]{2,1,0:T(8,128)S(1)}, f32[3,8,153]{2,1,0:T(8,128)S(1)}, u32[]{:S(2)}, u32[]{:S(2)}) collective-permute-start(f32[3,8,153]{2,1,0:T(8,128)S(1)} %pad_maximum_fusion.4), channel_id=1, source_target_pairs={{0,12},{4,0},{8,4},{12,8},{1,13},{5,1},{9,5},{13,9},{2,14},{6,2},{... | collective-permute-start | bytes 44072 | tf_op jit(solution)/shard_map/ppermute | solution.py:20
  84.6 1.2 collective-permute-start.14
  91.0 1.2 collective-permute-start.15
  92.4 5.6 %collective-permute-start.16 = (f32[3,8,153]{2,1,0:T(8,128)S(1)}, f32[3,8,153]{2,1,0:T(8,128)S(1)}, u32[]{:S(2)}, u32[]{:S(2)}) collective-permute-start(f32[3,8,153]{2,1,0:T(8,128)S(1)} %pad_maximum_fusion.5), channel_id=1, source_target_pairs={{0,4},{4,8},{8,12},{12,0},{1,5},{5,9},{9,13},{13,1},{2,6},{6,10},{... | collective-permute-start | bytes 44072 | tf_op jit(solution)/shard_map/ppermute | solution.py:20
  98.2 3.7 %collective-permute-start.17 = (f32[3,8,34]{2,1,0:T(8,128)S(1)}, f32[3,8,34]{2,1,0:T(8,128)S(1)}, u32[]{:S(2)}, u32[]{:S(2)}) collective-permute-start(f32[3,8,34]{2,1,0:T(8,128)S(1)} %pad_maximum_fusion.19), channel_id=1, source_target_pairs={{0,2},{2,0},{1,3},{3,1},{4,6},{6,4},{5,7},{7,5},{8,10},{10,8},{9,1... | collective-permute-start | bytes 9800 | tf_op jit(solution)/shard_map/ppermute | solution.py:20
  110.5 35.4 %copy-start.2 = (f32[3,8,128]{2,1,0:T(8,128)}, f32[3,8,128]{2,1,0:T(8,128)S(1)}, u32[]{:S(2)}) copy-start(f32[3,8,128]{2,1,0:T(8,128)S(1)} %pad_add_fusion) | copy-start | bytes 36868
  111.9 3.7 %collective-permute-start.18 = (f32[3,8,34]{2,1,0:T(8,128)S(1)}, f32[3,8,34]{2,1,0:T(8,128)S(1)}, u32[]{:S(2)}, u32[]{:S(2)}) collective-permute-start(f32[3,8,34]{2,1,0:T(8,128)S(1)} %pad_maximum_fusion.20), channel_id=1, source_target_pairs={{0,2},{2,0},{1,3},{3,1},{4,6},{6,4},{5,7},{7,5},{8,10},{10,8},{9,1... | collective-permute-start | bytes 9800 | tf_op jit(solution)/shard_map/ppermute | solution.py:20
  115.9 4.0 %collective-permute-start.19 = (f32[3,8,153]{2,1,0:T(8,128)S(1)}, f32[3,8,153]{2,1,0:T(8,128)S(1)}, u32[]{:S(2)}, u32[]{:S(2)}) collective-permute-start(f32[3,8,153]{2,1,0:T(8,128)S(1)} %pad_maximum_fusion.6), channel_id=1, source_target_pairs={{0,12},{4,0},{8,4},{12,8},{1,13},{5,1},{9,5},{13,9},{2,14},{6,2},{... | collective-permute-start | bytes 44072 | tf_op jit(solution)/shard_map/ppermute | solution.py:20
  120.1 1.2 collective-permute-start.20
  127.3 1.2 collective-permute-start.21
  128.8 5.6 %collective-permute-start.22 = (f32[3,8,153]{2,1,0:T(8,128)S(1)}, f32[3,8,153]{2,1,0:T(8,128)S(1)}, u32[]{:S(2)}, u32[]{:S(2)}) collective-permute-start(f32[3,8,153]{2,1,0:T(8,128)S(1)} %pad_maximum_fusion.7), channel_id=1, source_target_pairs={{0,4},{4,8},{8,12},{12,0},{1,5},{5,9},{9,13},{13,1},{2,6},{6,10},{... | collective-permute-start | bytes 44072 | tf_op jit(solution)/shard_map/ppermute | solution.py:20
  134.5 3.7 %collective-permute-start.23 = (f32[3,8,34]{2,1,0:T(8,128)S(1)}, f32[3,8,34]{2,1,0:T(8,128)S(1)}, u32[]{:S(2)}, u32[]{:S(2)}) collective-permute-start(f32[3,8,34]{2,1,0:T(8,128)S(1)} %pad_maximum_fusion.23), channel_id=1, source_target_pairs={{0,2},{2,0},{1,3},{3,1},{4,6},{6,4},{5,7},{7,5},{8,10},{10,8},{9,1... | collective-permute-start | bytes 9800 | tf_op jit(solution)/shard_map/ppermute | solution.py:20
